TPU v7x, 32 devices: a whole 2x2x4 slice. The times are simulated.
32 devices in a mesh: tp: 32 (over z, y, x, core).
Axes of the slice: x: 2, y: 2, z: 4, core: 2. Of those that a mesh axis runs over, the one named last changes fastest.
Arguments:
- hidden: bfloat16 [3, 2048, 4096], P(None, 'tp')
- labels: int32 [3, 2048], P(None, 'tp')
- loss_mask: int32 [3, 2048], P(None, 'tp')
- norm_gain: float32 [4096], replicated
- w_head: bfloat16 [4096, 65536], P(None, 'tp')
Outputs:
- output 1: float32 [], replicated
- output 2: bfloat16 [3, 2048, 4096], P(None, 'tp')
- output 3: bfloat16 [4096, 65536], P(None, 'tp')
- output 4: float32 [4096], replicated
All inputs are finite; a program needn't handle non-finite values.
Results may differ from a plain program's by a relative error of at most 0.00839355.
Values are sent between devices in bfloat16 or wider.
A program may use at most 1 GiB of HBM per device.

v0:
```python
import jax
import jax.numpy as jnp
from jax import lax
from jax.sharding import PartitionSpec as P, NamedSharding

NORM_EPS = 1e-6


def rms_norm(x_rows, norm_gain):
    inv_rms = lax.rsqrt(jnp.mean(x_rows * x_rows, axis=-1, keepdims=True) + NORM_EPS)
    return x_rows * inv_rms * norm_gain


def solution(mesh):
    n_shards = mesh.shape['tp']

    def device_step(hidden, labels, loss_mask, norm_gain, w_head):
        batch_size, seq_loc, model_width = hidden.shape
        v_loc = w_head.shape[1]
        norm_loc, norm_vjp = jax.vjp(rms_norm, hidden.astype(jnp.float32), norm_gain)
        hn_all = lax.all_gather(norm_loc.astype(jnp.bfloat16), 'tp', axis=1, tiled=True)
        label_all = lax.all_gather(labels, 'tp', axis=1, tiled=True)
        mask_all = lax.all_gather(loss_mask, 'tp', axis=1, tiled=True)
        logits = jnp.einsum('btd,dv->btv', hn_all, w_head, preferred_element_type=jnp.float32)
        row_max = lax.pmax(jnp.max(logits, axis=-1), 'tp')
        sum_exp = lax.psum(jnp.sum(jnp.exp(logits - row_max[..., None]), axis=-1), 'tp')
        col_start = lax.axis_index('tp') * v_loc
        is_label = (lax.broadcasted_iota(jnp.int32, (1, 1, v_loc), 2) + col_start) == label_all[..., None]
        label_logit = lax.psum(jnp.sum(jnp.where(is_label, logits, 0.0), axis=-1), 'tp')
        log_norm = row_max + jnp.log(sum_exp)
        tok_weight = mask_all.astype(jnp.float32)
        kept_count = jnp.sum(tok_weight)
        mean_loss = jnp.sum(tok_weight * (log_norm - label_logit)) / kept_count
        tok_scale = tok_weight / kept_count
        d_logits = ((jnp.exp(logits - log_norm[..., None]) - is_label.astype(jnp.float32)) * tok_scale[..., None]).astype(jnp.bfloat16)
        d_head = jnp.einsum('btd,btv->dv', hn_all, d_logits, preferred_element_type=jnp.float32).astype(jnp.bfloat16)
        dhn_part = jnp.einsum('btv,dv->btd', d_logits, w_head, preferred_element_type=jnp.float32).astype(jnp.bfloat16)
        received = lax.all_to_all(dhn_part.reshape(batch_size, n_shards, seq_loc, model_width), 'tp', 1, 1, tiled=True)
        d_norm = jnp.sum(received, axis=1, dtype=jnp.float32)
        d_x, d_gain = norm_vjp(d_norm)
        d_gain = lax.psum(d_gain, 'tp')
        return mean_loss, d_x.astype(jnp.bfloat16), d_head, d_gain

    return jax.shard_map(device_step, mesh=mesh, in_specs=(P(None, 'tp', None), P(None, 'tp'), P(None, 'tp'), P(), P(None, 'tp')), out_specs=(P(), P(None, 'tp', None), P(None, 'tp'), P()), check_vma=False)
```

profile of v0, /device:TPU:0, one launch (start us, length us, event | category | flops | bytes accessed | tf_op | source)
XLA Modules:
  0.0 1873.2 jit_solution(2860485314141947943)
XLA Ops:
  7.2 1.8 fusion.12
  9.6 0.6 copy-done.6
  10.2 3.0 fusion.9
  13.2 45.4 %all-gather = s32[32,64,3]{1,2,0:T(4,128)S(1)} all-gather(s32[1,64,3]{1,2,0:T(4,128)} %bitcast.36), channel_id=1, replica_groups=mesh['tp'=32] {'tp'}, dimensions={0}, use_global_device_ids=true | all-gather | bytes 25344 | tf_op jit(solution)/shard_map/all_gather | solution.py:23
  58.7 38.4 %all-gather.1 = s32[32,64,3]{1,2,0:T(4,128)S(1)} all-gather(s32[1,64,3]{1,2,0:T(4,128)} %bitcast.37), channel_id=1, replica_groups=mesh['tp'=32] {'tp'}, dimensions={0}, use_global_device_ids=true | all-gather | bytes 25344 | tf_op jit(solution)/shard_map/all_gather | solution.py:22
  97.1 0.7 reshape.44
  97.8 0.6 iota_add_fusion
  98.4 0.6 convert_reduce_fusion.1
  99.0 1.3 bitcast_divide_fusion
  100.3 191.2 %all-gather.4.cloned.1.call-done = bf16[3,2048,4096]{2,1,0:T(8,128)(2,1)} async-done(((bf16[3,64,4096]{2,1,0:T(8,128)(2,1)}), bf16[3,2048,4096]{2,1,0:T(8,128)(2,1)}) %all-gather.4.cloned.1.call-update) | async-done | bytes 50331664 | tf_op jit(solution)/shard_map/all_gather | solution.py:21
  291.5 116.4 %fusion.18 = (f32[3,2048]{1,0:T(4,128)S(1)}, f32[3,2048,2048]{1,2,0:T(8,128)}) fusion(bf16[3,2048,4096]{2,1,0:T(8,128)(2,1)} %all-gather.4.cloned.1.call-done, bf16[4096,2048]{1,0:T(8,128)(2,1)} %param.9), kind=kOutput, calls=%fused_computation.34 | convolution fusion | flops 103091789824 | bytes 117465088 | tf_op jit(solution)/shard_map/btd,dv->btv/dot_general | solution.py:24
  408.0 38.5 %pmax.7 = f32[3,2048]{1,0:T(4,128)S(1)} all-reduce(f32[3,2048]{1,0:T(4,128)S(1)} %get-tuple-element.10), channel_id=1, replica_groups=mesh['tp'=32] {'tp'}, use_global_device_ids=true, to_apply=%region_2.0 | all-reduce | flops 6144 | bytes 49152 | tf_op jit(solution)/shard_map/pmax | solution.py:25
  446.5 23.2 %fusion = (f32[3,2048]{1,0:T(4,128)}, f32[3,2048]{1,0:T(4,128)S(1)}) fusion(f32[3,2048,2048]{1,2,0:T(8,128)} %get-tuple-element.11, s32[3,2048]{1,0:T(4,128)S(1)} %bitcast.33, s32[2048]{0:T(1024)S(1)} %copy-done.8, f32[3,2048]{1,0:T(4,128)S(1)} %pmax.7), kind=kLoop, calls=%fused_computation.3 | loop fusion | flops 62902272 | bytes 50438144 | tf_op jit(solution)/shard_map/reduce_sum | solution.py:29
  469.7 41.0 %psum.21 = f32[3,2048]{1,0:T(4,128)S(1)} all-reduce(f32[3,2048]{1,0:T(4,128)S(1)} %get-tuple-element.5), channel_id=1, replica_groups=mesh['tp'=32] {'tp'}, use_global_device_ids=true, to_apply=%region_4.0 | all-reduce | flops 6144 | bytes 49152 | tf_op jit(solution)/shard_map/psum | solution.py:26
  510.7 126.4 %convolution_convert_fusion = bf16[3,2048,4096]{2,1,0:T(8,128)(2,1)} fusion(bf16[4096,2048]{1,0:T(8,128)(2,1)} %param.9, f32[3,2048,2048]{1,2,0:T(8,128)} %get-tuple-element.11, f32[3,2048]{1,0:T(4,128)S(1)} %copy-done.5, f32[3,2048]{1,0:T(4,128)S(1)} %log_add_fusion, s32[3,2048]{1,0:T(4,128)S(1)} %bitcast.34, s32[2048]{0:T(1024)S(1)} %copy-done.8), kind=kOutput, calls=%fused_computation.9 | convolution fusion | flops 103179878400 | bytes 117522432 | tf_op jit(solution)/shard_map/btv,dv->btd/dot_general | solution.py:37
  637.1 33.8 %copy.21 = bf16[3,32,64,4096]{3,2,0,1:T(8,128)(2,1)} copy(bf16[3,32,64,4096]{3,2,1,0:T(8,128)(2,1)} %bitcast.32) | data formatting | bytes 100663296 | tf_op jit(solution)/shard_map/reshape | solution.py:38
  670.9 4.9 all-to-all-start
  675.8 126.4 %bitcast_convert_fusion = bf16[4096,2048]{1,0:T(8,128)(2,1)} fusion(bf16[3,2048,4096]{2,1,0:T(8,128)(2,1)} %all-gather.4.cloned.1.call-done, f32[3,2048,2048]{1,2,0:T(8,128)} %get-tuple-element.11, f32[3,2048]{1,0:T(4,128)S(1)} %copy-done.5, f32[3,2048]{1,0:T(4,128)S(1)} %log_add_fusion, s32[3,2048]{1,0:T(4,128)S(1)} %bitcast.35, s32[2048]{0:T(1024)S(1)} %copy-done.8), kind=kOutput, calls=%fused_computation.8 | convolution fusion | flops 103163101184 | bytes 117522432 | tf_op jit(solution)/shard_map/btd,btv->dv/dot_general | solution.py:36
  802.2 1001.1 %all-to-all-done = bf16[3,32,64,4096]{3,2,0,1:T(8,128)(2,1)} async-done(((bf16[3,32,64,4096]{3,2,0,1:T(8,128)(2,1)}), bf16[3,32,64,4096]{3,2,0,1:T(8,128)(2,1)}, u32[]{:S(2)}, u32[]{:S(2)}) %all-to-all-start) | async-done | bytes 50331680 | tf_op jit(solution)/shard_map/all_to_all | solution.py:38
  1803.3 16.1 convert_reduce_fusion
  1819.5 2.5 fusion.10
  1822.0 3.4 fusion.11
  1825.4 37.7 %all-reduce = (f32[3,2048]{1,0:T(4,128)S(1)}, f32[4096]{0:T(1024)}) all-reduce(f32[3,2048]{1,0:T(4,128)S(1)} %copy-done.3, f32[4096]{0:T(1024)S(1)} %get-tuple-element.6), channel_id=1, replica_groups=mesh['tp'=32] {'tp'}, use_global_device_ids=true, to_apply=%region_6.7 | all-reduce | flops 10240 | bytes 81920 | tf_op jit(solution)/shard_map/psum | solution.py:29
  1863.1 0.7 fusion.14
  (30 shorter events, 0.8 us)
Async XLA Ops:
  7.2 284.4 %all-gather.4.cloned.1.call-start = ((), (), s32[]{:S(2)}) async-start(), calls=%async_computation.1 | async-start | bytes 51904512 | tf_op jit(solution)/shard_map/all_gather | solution.py:21
  9.0 0.6 copy-start.9
  9.6 0.6 copy-start.6
  58.7 349.3 %copy-start = (f32[2048,3]{0,1:T(4,128)}, f32[2048,3]{0,1:T(4,128)S(1)}, u32[]{:S(2)}) copy-start(f32[2048,3]{0,1:T(4,128)S(1)} %reshape.45) | copy-start | bytes 73732
  291.5 155.0 %copy-start.4 = (s32[2048,3]{0,1:T(4,128)S(1)}, s32[2048,3]{0,1:T(4,128)}, u32[]{:S(2)}) copy-start(s32[2048,3]{0,1:T(4,128)} %reshape.44) | copy-start | bytes 73732
  291.5 155.0 %copy-start.8 = (s32[2048]{0:T(1024)S(1)}, s32[2048]{0:T(1024)}, u32[]{:S(2)}) copy-start(s32[2048]{0:T(1024)} %iota_add_fusion) | copy-start | bytes 24580
  446.5 64.2 %copy-start.5 = (f32[3,2048]{1,0:T(4,128)S(1)}, f32[3,2048]{1,0:T(4,128)}, u32[]{:S(2)}) copy-start(f32[3,2048]{1,0:T(4,128)} %bitcast_divide_fusion) | copy-start | bytes 73732
  670.9 1132.4 %all-to-all-start = ((bf16[3,32,64,4096]{3,2,0,1:T(8,128)(2,1)}), bf16[3,32,64,4096]{3,2,0,1:T(8,128)(2,1)}, u32[]{:S(2)}, u32[]{:S(2)}) async-start(bf16[3,32,64,4096]{3,2,0,1:T(8,128)(2,1)} %copy.21), calls=%async_computation | async-start | bytes 100663296 | tf_op jit(solution)/shard_map/all_to_all | solution.py:38
  802.2 1017.2 %copy-start.2 = (f32[4096]{0:T(1024)S(1)}, f32[4096]{0:T(1024)}, u32[]{:S(2)}) copy-start(f32[4096]{0:T(1024)} %param.8) | copy-start | bytes 49156
  802.2 1017.3 %copy-start.7 = (f32[3,64]{1,0:T(4,128)S(1)}, f32[3,64]{1,0:T(4,128)}, u32[]{:S(2)}) copy-start(f32[3,64]{1,0:T(4,128)} %copy-done.6) | copy-start | bytes 2308
  802.2 1019.8 %copy-start.10 = (f32[3,64]{1,0:T(4,128)S(1)}, f32[3,64]{1,0:T(4,128)}, u32[]{:S(2)}) copy-start(f32[3,64]{1,0:T(4,128)} %copy-done.9) | copy-start | bytes 2308
  802.2 1023.2 %copy-start.3 = (f32[3,2048]{1,0:T(4,128)S(1)}, f32[3,2048]{1,0:T(4,128)}, u32[]{:S(2)}) copy-start(f32[3,2048]{1,0:T(4,128)} %get-tuple-element.4) | copy-start | bytes 73732
  802.2 1060.9 %copy-start.1 = (f32[2048,3]{0,1:T(4,128)S(1)}, f32[2048,3]{0,1:T(4,128)}, u32[]{:S(2)}) copy-start(f32[2048,3]{0,1:T(4,128)} %copy-done) | copy-start | bytes 73732
Sparse Core Ops, SparseCore 0:
  13.3 278.1 all-gather.3
where the time goes:
time: 1870 us
  waiting for transfers between devices  1190 us (64%)
  matrix products  369 us (20%)
  blocking collectives  201 us (11%)
  other arithmetic  53.2 us (3%)
  local copies, waits for them, and re-layouts  35.8 us (2%)
    all_to_all x1, waiting for transfers between devices, device_step(): lax.all_to_all(dhn_part.reshape(batch_size, n_shards, seq_loc, model_widt...  1000 us
    all_gather x1, waiting for transfers between devices, device_step(): lax.all_gather(norm_loc.astype(jnp.bfloat16), 'tp', axis=1, tiled=True)  191 us
    dot_general x1, matrix products, device_step(): jnp.einsum('btd,btv->dv', hn_all, d_logits, preferred_element_type=jnp.fl...  126 us
    dot_general x1, matrix products, device_step(): jnp.einsum('btv,dv->btd', d_logits, w_head, preferred_element_type=jnp.fl...  126 us
    dot_general x1, matrix products, device_step(): jnp.einsum('btd,dv->btv', hn_all, w_head, preferred_element_type=jnp.floa...  116 us
    all_gather x1, blocking collectives, device_step(): mask_all = lax.all_gather(loss_mask, 'tp', axis=1, tiled=True)  45.4 us
    psum x1, blocking collectives, device_step(): lax.psum(jnp.sum(jnp.exp(logits - row_max[..., None]), axis=-1), 'tp')  41 us
    pmax x1, blocking collectives, device_step(): row_max = lax.pmax(jnp.max(logits, axis=-1), 'tp')  38.5 us
  transfers between devices with their start and end apart: 2, of which 2 were waited for; matrix products, arithmetic and copies ran while one was open for 7% of the time, Pallas kernels for 0%

commit v1 on v0

v1 whole, which is shorter than its diff:
```python
import jax
import jax.numpy as jnp
from jax import lax
from jax.sharding import PartitionSpec as P

NORM_EPS = 1e-6
STAGES = ((1, 96), (2, 64), (4, 48), (8, 32))
ROWS = 128
CHUNKS = 2
UNITS = ((('y', 'z', 'x'), 6), (('x', 'z', 'y'), 6), (('x', 'y', 'z'), 10), (('y', 'x', 'z'), 10))


def rms_norm(x_rows, norm_gain):
    inv_rms = lax.rsqrt(jnp.mean(x_rows * x_rows, axis=-1, keepdims=True) + NORM_EPS)
    return x_rows * inv_rms * norm_gain


def full_step(n_shards, hidden, labels, loss_mask, norm_gain, w_head):
    batch_size, seq_loc, model_width = hidden.shape
    v_loc = w_head.shape[1]
    norm_loc, norm_vjp = jax.vjp(rms_norm, hidden.astype(jnp.float32), norm_gain)
    hn_all = lax.all_gather(norm_loc.astype(jnp.bfloat16), 'tp', axis=1, tiled=True)
    label_all = lax.all_gather(labels, 'tp', axis=1, tiled=True)
    mask_all = lax.all_gather(loss_mask, 'tp', axis=1, tiled=True)
    logits = jnp.einsum('btd,dv->btv', hn_all, w_head, preferred_element_type=jnp.float32)
    row_max = lax.pmax(jnp.max(logits, axis=-1), 'tp')
    sum_exp = lax.psum(jnp.sum(jnp.exp(logits - row_max[..., None]), axis=-1), 'tp')
    col_start = lax.axis_index('tp') * v_loc
    is_label = (lax.broadcasted_iota(jnp.int32, (1, 1, v_loc), 2) + col_start) == label_all[..., None]
    label_logit = lax.psum(jnp.sum(jnp.where(is_label, logits, 0.0), axis=-1), 'tp')
    log_norm = row_max + jnp.log(sum_exp)
    tok_weight = mask_all.astype(jnp.float32)
    kept_count = jnp.sum(tok_weight)
    mean_loss = jnp.sum(tok_weight * (log_norm - label_logit)) / kept_count
    tok_scale = tok_weight / kept_count
    d_logits = ((jnp.exp(logits - log_norm[..., None]) - is_label.astype(jnp.float32)) * tok_scale[..., None]).astype(jnp.bfloat16)
    d_head = jnp.einsum('btd,btv->dv', hn_all, d_logits, preferred_element_type=jnp.float32).astype(jnp.bfloat16)
    dhn_part = jnp.einsum('btv,dv->btd', d_logits, w_head, preferred_element_type=jnp.float32).astype(jnp.bfloat16)
    received = lax.all_to_all(dhn_part.reshape(batch_size, n_shards, seq_loc, model_width), 'tp', 1, 1, tiled=True)
    d_norm = jnp.sum(received, axis=1, dtype=jnp.float32)
    d_x, d_gain = norm_vjp(d_norm)
    d_gain = lax.psum(d_gain, 'tp')
    return mean_loss, d_x.astype(jnp.bfloat16), d_head, d_gain


def solution(mesh):
    n = mesh.shape['tp']
    dims = (n // 8, 2, 2, 2)
    bits = [1 << i for i in range(n.bit_length() - 1)]

    def swap(a, flip):
        return lax.ppermute(a, 'tp', [(i, i ^ flip) for i in range(n)])

    def at(a, axis, i):
        return lax.dynamic_index_in_dim(a, i, axis, keepdims=False)

    def after(values, dep):
        return lax.optimization_barrier((values, dep))[0]

    def device_step(hidden, labels, loss_mask, norm_gain, w_head):
        f32, i32 = jnp.float32, jnp.int32
        batch_size, seq_loc, model_width = hidden.shape
        n_rows = batch_size * seq_loc
        v_loc = w_head.shape[1]
        me = lax.axis_index('tp')
        place = {'core': me & 1, 'x': (me >> 1) & 1, 'y': (me >> 2) & 1, 'z': me >> 3}
        slot = jnp.arange(n_rows, dtype=i32)

        mask = loss_mask.reshape(n_rows)
        pos = jnp.cumsum(mask) - 1
        count = jnp.sum(mask)
        chosen = (pos[None, :] == slot[:, None]) & (mask[None, :] == 1)
        order = jnp.sum(jnp.where(chosen, slot[None, :], 0), axis=1)
        lab = jnp.sum(jnp.where(chosen, labels.reshape(n_rows)[None, :], 0), axis=1)
        rows = jnp.take(hidden.reshape(n_rows, model_width), order, axis=0, mode='clip')
        fits = jnp.bool_(True)
        moves = []
        for bit, cap in STAGES:
            start = jnp.maximum(count - cap, 0)
            ints = jnp.concatenate([lax.dynamic_slice_in_dim(lab, start, cap), jnp.full((128,), count, i32)])
            got_rows = swap(lax.dynamic_slice_in_dim(rows, start, cap), bit)
            got_ints = swap(ints, bit)
            other = got_ints[cap]
            upper = (me & bit) // bit
            target = (count + other + 1 - upper) >> 1
            fits = fits & (jnp.abs(target - count) <= cap)
            first = count + other - target - jnp.maximum(other - cap, 0)
            src = jnp.where(slot < count, slot, n_rows + jnp.clip(first + slot - count, 0, cap - 1))
            rows = jnp.take(jnp.concatenate([rows, got_rows]), src, axis=0, mode='clip')
            lab = jnp.take(jnp.concatenate([lab, got_ints[:cap]]), src, axis=0, mode='clip')
            moves.append((bit, cap, count, other, target))
            count = target
        fits = fits & (count <= ROWS)
        x_rows, lab = rows[:ROWS], jnp.where(slot < count, lab, -1)[:ROWS]

        norm_loc, norm_vjp = jax.vjp(rms_norm, x_rows.astype(f32), norm_gain)
        hn_loc = norm_loc.astype(jnp.bfloat16)
        per = ROWS // CHUNKS
        hn = [lax.all_gather(hn_loc[c * per:(c + 1) * per], 'tp', axis=0, tiled=True) for c in range(CHUNKS)]
        known = lax.all_gather(jnp.concatenate([lab, jnp.full((128,), fits.astype(i32))]), 'tp', axis=0, tiled=False)
        all_fit = jnp.min(known[:, ROWS]) == 1
        label_all = [known[:, c * per:(c + 1) * per].reshape(n * per) for c in range(CHUNKS)]
        weight = [(lb >= 0).astype(f32) for lb in label_all]
        kept_count = sum(jnp.sum(w) for w in weight)
        cols = lax.broadcasted_iota(i32, (1, v_loc), 1) + me * v_loc

        def forward(c):
            lg = jnp.einsum('td,dv->tv', hn[c], w_head, preferred_element_type=f32)
            lg = lax.optimization_barrier(lg)
            row_max = jnp.max(lg, axis=-1)
            row_sum = jnp.sum(jnp.exp(lg - row_max[:, None]), axis=-1)
            row_lab = jnp.sum(jnp.where(cols == label_all[c][:, None], lg, 0.0), axis=-1)
            return lg, jnp.stack([row_max, row_sum, row_lab])

        def combine(mine):
            for bit in bits:
                theirs = swap(mine, bit)
                upper = (me & bit) != 0
                lo, hi = jnp.where(upper, theirs, mine), jnp.where(upper, mine, theirs)
                top = jnp.maximum(lo[0], hi[0])
                mine = jnp.stack([top, lo[1] * jnp.exp(lo[0] - top) + hi[1] * jnp.exp(hi[0] - top), lo[2] + hi[2]])
            return mine[0] + jnp.log(mine[1]), mine[2]

        def softmax_grad(c, lg, log_norm):
            is_label = (cols == label_all[c][:, None]).astype(f32)
            scale = weight[c] / kept_count
            return ((jnp.exp(lg - log_norm[:, None]) - is_label) * scale[:, None]).astype(jnp.bfloat16)

        class Reduce:
            def __init__(self, part, path):
                part = part.reshape(*dims, per, -1)
                step = {'x': 2, 'y': 4}
                a, self.second_axis, self.third_axis = path
                a_axis = {'y': 1, 'x': 2}[a]
                self.bit = {**step, 'z': 8}

                def group(da, dc):
                    return at(at(part, 3, place['core'] ^ dc), a_axis, place[a] ^ da)

                self.sent = [group(1, 0), group(1, 1), group(0, 1)]
                self.terms = [group(0, 0)]
                self.terms += [swap(g, f) for g, f in zip(self.sent, (step[a], step[a] | 1, 1))]

            def _exchange(self, pick, name):
                size = dims[0] if name == 'z' else 2
                self.sent = [pick(place[name] ^ d) for d in range(1, size)]
                self.terms = [pick(place[name])]
                self.terms += [swap(g, self.bit[name] * d) for d, g in enumerate(self.sent, 1)]
                return self.sent

            def second(self, dep):
                terms, name = after(self.terms, dep), self.second_axis
                axis = 0 if name == 'z' else 1
                return self._exchange(lambda i: sum(at(t, axis, i).astype(f32) for t in terms), name)

            def third(self, dep):
                terms = after(self.terms, dep)
                return self._exchange(lambda i: sum(at(t, 0, i) for t in terms), self.third_axis)

            def last(self, dep):
                return sum(after(self.terms, dep))

        d_logits, log_norm, label_logit, units = {}, {}, {}, {}

        def hidden_grad(c, u, dep):
            low = sum(w for _, w in UNITS[:u]) * model_width // 32
            path, w = UNITS[u]
            dl, w_part = after(d_logits[c], dep), w_head[low:low + w * model_width // 32]
            part = jnp.einsum('tv,dv->td', dl, w_part, preferred_element_type=f32).astype(jnp.bfloat16)
            units[c, u] = Reduce(part, path)
            return units[c, u].sent

        def head_grad(c, acc, dep):
            dl = after(d_logits[c], dep)
            term = jnp.einsum('td,tv->dv', hn[c], dl, preferred_element_type=f32)
            return term if acc is None else acc + term

        nu = len(UNITS)
        lg0, st0 = forward(0)
        log_norm[0], label_logit[0] = combine(st0)
        d_logits[0] = softmax_grad(0, lg0, log_norm[0])
        dep = d_logits[0]
        for u in range(nu):
            dep = hidden_grad(0, u, dep)
        hn[1] = after(hn[1], dep)
        lg1, st1 = forward(1)
        for u in range(2):
            dep = units[0, u].second(st1)
        log_norm[1], label_logit[1] = combine(after(st1, dep))
        lg1 = after(lg1, log_norm[1])
        d_logits[1] = dep = softmax_grad(1, lg1, log_norm[1])
        for u in range(2, nu):
            dep = units[0, u].second(dep)
        for u in range(nu):
            dep = hidden_grad(1, u, dep)
        for u in range(2):
            dep = units[0, u].third(dep)
        head = dep = head_grad(0, None, dep)
        for u in range(2):
            dep = units[1, u].second(dep)
        for u in range(2, nu):
            dep = units[0, u].third(dep)
        for u in range(2, nu):
            dep = units[1, u].second(dep)
        d_head = dep = head_grad(1, head, dep).astype(jnp.bfloat16)
        for u in range(nu):
            dep = units[1, u].third(dep)
        d_norm = jnp.concatenate([jnp.concatenate([units[c, u].last(dep) for u in range(nu)], axis=-1) for c in range(CHUNKS)])
        loss = sum(jnp.sum(weight[c] * (log_norm[c] - label_logit[c])) for c in range(CHUNKS))
        mean_loss = loss / kept_count
        d_x, d_gain = norm_vjp(d_norm)
        for bit in bits:
            d_gain = d_gain + swap(d_gain, bit)

        back = jnp.concatenate([d_x.astype(jnp.bfloat16), jnp.zeros((n_rows - ROWS, model_width), jnp.bfloat16)])
        for bit, cap, count, other, target in reversed(moves):
            got = swap(lax.dynamic_slice_in_dim(back, jnp.minimum(count, n_rows - cap), cap), bit)
            first = jnp.maximum(other - (n_rows - cap), 0)
            src = jnp.where(slot < target, slot, n_rows + jnp.clip(first + slot - target, 0, cap - 1))
            back = jnp.take(jnp.concatenate([back, got]), src, axis=0, mode='clip')
        back = jnp.where(mask[:, None] == 1, jnp.take(back, pos, axis=0, mode='clip'), jnp.zeros((), jnp.bfloat16))
        d_hidden = back.reshape(hidden.shape)
        return lax.cond(
            all_fit,
            lambda: (mean_loss, d_hidden, d_head, d_gain),
            lambda: full_step(n, hidden, labels, loss_mask, norm_gain, w_head),
        )

    return jax.shard_map(device_step, mesh=mesh, in_specs=(P(None, 'tp', None), P(None, 'tp'), P(None, 'tp'), P(), P(None, 'tp')), out_specs=(P(), P(None, 'tp', None), P(None, 'tp'), P()), check_vma=False)
```

time: 1870 us -> 1030 us (0.55)
  waiting for transfers between devices: 1190 us -> 370 us
  blocking collectives: 201 us -> 42.3 us
  starting transfers between devices: 4.92 us -> 116 us
  matrix products: 369 us -> 268 us
  other arithmetic: 53.2 us -> 115 us
  local copies, waits for them, and re-layouts: 35.8 us -> 74 us
    all_to_all x1 -> x0, waiting for transfers between devices: 1000 us -> none  [device_step(): lax.all_to_all(dhn_part.reshape(batch_size, n_shards, seq_loc, model_widt...]
    ppermute x0 -> x83, waiting for transfers between devices: none -> 300 us  [swap(): return lax.ppermute(a, 'tp', [(i, i ^ flip) for i in range(n)])]
    all_gather x1 -> x2, waiting for transfers between devices: 191 us -> 69.8 us  [device_step(): lax.all_gather(hn_loc[c * per:(c + 1) * per], 'tp', axis=0, tiled=True)]
    ppermute x0 -> x83, starting transfers between devices: none -> 116 us  [swap(): return lax.ppermute(a, 'tp', [(i, i ^ flip) for i in range(n)])]
    dot_general x3 -> x12, matrix products: 369 us -> 268 us  [the longest x8 93.7 us: hidden_grad(): jnp.einsum('tv,dv->td', dl, w_part, preferred_element_type=f32)]
    psum x2 -> x0, blocking collectives: 78.7 us -> none  [the longest x1 41 us: device_step(): lax.psum(jnp.sum(jnp.exp(logits - row_max[..., None]), axis=-1), 'tp')]
    all_gather x2 -> x1, blocking collectives: 83.7 us -> 42.3 us  [device_step(): lax.all_gather(jnp.concatenate([lab, jnp.full((128,), fits.astype(i32))])...]
    add x2 -> x42, other arithmetic: 0.62 us -> 40.4 us  [the longest x8 24.6 us: second(): sum((at(t, axis, i).astype(f32) for t in terms))]
  transfers between devices with their start and end apart: 2 -> 85, of which waited for: 2 -> 38; matrix products, arithmetic and copies ran while one was open for 7% -> 38% of each run, Pallas kernels for 0% -> 0%
where the time goes in v1:
time: 1030 us; the launch traced here: 1020 us
  waiting for transfers between devices  370 us (36%)
  matrix products  268 us (26%)
  starting transfers between devices  116 us (11%)
  other arithmetic  115 us (11%)
  local copies, waits for them, and re-layouts  74 us (7%)
  blocking collectives  42.3 us (4%)
  between operations  29.1 us (3%)
    ppermute x83, waiting for transfers between devices, swap(): return lax.ppermute(a, 'tp', [(i, i ^ flip) for i in range(n)])  300 us
    ppermute x83, starting transfers between devices, swap(): return lax.ppermute(a, 'tp', [(i, i ^ flip) for i in range(n)])  116 us
    dot_general x8, matrix products, hidden_grad(): jnp.einsum('tv,dv->td', dl, w_part, preferred_element_type=f32)  93.7 us
    dot_general x2, matrix products, head_grad(): term = jnp.einsum('td,tv->dv', hn[c], dl, preferred_element_type=f32)  88.1 us
    dot_general x2, matrix products, forward(): lg = jnp.einsum('td,dv->tv', hn[c], w_head, preferred_element_type=f32)  86.1 us
    all_gather x2, waiting for transfers between devices, device_step(): lax.all_gather(hn_loc[c * per:(c + 1) * per], 'tp', axis=0, tiled=True)  69.8 us
    all_gather x1, blocking collectives, device_step(): lax.all_gather(jnp.concatenate([lab, jnp.full((128,), fits.astype(i32))])...  42.3 us
    add x8, other arithmetic, second(): sum((at(t, axis, i).astype(f32) for t in terms))  24.6 us
  transfers between devices with their start and end apart: 85, of which 38 were waited for; matrix products, arithmetic and copies ran while one was open for 38% of the time, Pallas kernels for 0%

profile of v1, /device:TPU:0, one launch (start us, length us, event | category | flops | bytes accessed | tf_op | source)
XLA Modules:
  0.0 1020.5 jit_solution(11211649227447950385)
XLA Ops:
  82.4 42.3 %all-gather.3 = s32[32,1,256]{2,1,0:T(1,128)S(1)} all-gather(s32[1,1,256]{2,1,0:T(1,128)S(1)} %bitcast.321), channel_id=2, replica_groups=mesh['tp'=32] {'tp'}, dimensions={0}, use_global_device_ids=true | all-gather | bytes 33792 | tf_op jit(solution)/shard_map/all_gather | solution.py:100
  124.9 69.8 %all-gather.10.cloned.1.call-done = bf16[2048,4096]{1,0:T(8,128)(2,1)} async-done(((bf16[64,4096]{1,0:T(8,128)(2,1)}), bf16[2048,4096]{1,0:T(8,128)(2,1)}) %all-gather.10.cloned.1.call-update) | async-done | bytes 16777232 | tf_op jit(solution)/shard_map/all_gather | solution.py:99
  194.7 43.0 %fusion.66 = f32[2048,2048]{1,0:T(8,128)} fusion(bf16[2048,4096]{1,0:T(8,128)(2,1)} %all-gather.10.cloned.1.call-done, bf16[4096,2048]{1,0:T(8,128)(2,1)} %param.11), kind=kOutput, calls=%fused_computation.350 | convolution fusion | flops 34359738368 | bytes 50331648 | tf_op jit(solution)/shard_map/td,dv->tv/dot_general | solution.py:108
  311.1 13.7 %convolution_convert_fusion.4 = bf16[2048,1280]{1,0:T(8,128)(2,1)S(1)} fusion(bf16[2048,2048]{1,0:T(8,128)(2,1)S(1)} %fusion.25, bf16[4096,2048]{1,0:T(8,128)(2,1)} %param.11), kind=kOutput, calls=%fused_computation.81 | convolution fusion | flops 10740039680 | bytes 18874368 | tf_op jit(solution)/shard_map/tv,dv->td/dot_general | solution.py:169
  328.8 14.1 %convolution_convert_fusion.3 = bf16[2048,1280]{1,0:T(8,128)(2,1)S(1)} fusion(bf16[2048,2048]{1,0:T(8,128)(2,1)S(1)} %fusion.25, bf16[4096,2048]{1,0:T(8,128)(2,1)} %param.11), kind=kOutput, calls=%fused_computation.80 | convolution fusion | flops 10740039680 | bytes 18874368 | tf_op jit(solution)/shard_map/tv,dv->td/dot_general | solution.py:169
  346.9 43.0 %fusion.67 = f32[2048,2048]{1,0:T(8,128)} fusion(bf16[2048,4096]{1,0:T(8,128)(2,1)} %all-gather.12.cloned.1.call-done, bf16[4096,2048]{1,0:T(8,128)(2,1)} %param.11), kind=kOutput, calls=%fused_computation.351 | convolution fusion | flops 34359738368 | bytes 50331648 | tf_op jit(solution)/shard_map/td,dv->tv/dot_general | solution.py:108
  422.5 14.5 %collective-permute-done.22 = bf16[4,2,64,768]{3,2,1,0:T(8,128)(2,1)S(1)} collective-permute-done((bf16[4,2,64,768]{3,2,1,0:T(8,128)(2,1)S(1)}, bf16[4,2,64,768]{3,2,1,0:T(8,128)(2,1)S(1)}, u32[]{:S(2)}, u32[]{:S(2)}) %collective-permute-start.22) | collective-permute-done | bytes 786464 | tf_op jit(solution)/shard_map/ppermute | solution.py:52
  438.3 16.1 %collective-permute-done.21 = bf16[4,2,64,768]{3,2,1,0:T(8,128)(2,1)S(1)} collective-permute-done((bf16[4,2,64,768]{3,2,1,0:T(8,128)(2,1)S(1)}, bf16[4,2,64,768]{3,2,1,0:T(8,128)(2,1)S(1)}, u32[]{:S(2)}, u32[]{:S(2)}) %collective-permute-start.21) | collective-permute-done | bytes 786464 | tf_op jit(solution)/shard_map/ppermute | solution.py:52
  486.1 25.5 %collective-permute-done.28 = bf16[4,2,64,1280]{3,2,0,1:T(8,128)(2,1)} collective-permute-done((bf16[4,2,64,1280]{3,2,0,1:T(8,128)(2,1)S(1)}, bf16[4,2,64,1280]{3,2,0,1:T(8,128)(2,1)}, u32[]{:S(2)}, u32[]{:S(2)}) %collective-permute-start.28) | collective-permute-done | bytes 1310752 | tf_op jit(solution)/shard_map/ppermute | solution.py:52
  540.5 13.7 %convolution_convert_fusion.2 = bf16[2048,1280]{1,0:T(8,128)(2,1)S(1)} fusion(bf16[2048,2048]{1,0:T(8,128)(2,1)S(1)} %fusion.29, bf16[4096,2048]{1,0:T(8,128)(2,1)} %param.11), kind=kOutput, calls=%fused_computation.79 | convolution fusion | flops 10740039680 | bytes 18874368 | tf_op jit(solution)/shard_map/tv,dv->td/dot_general | solution.py:169
  577.2 13.7 %convolution_convert_fusion.1 = bf16[2048,1280]{1,0:T(8,128)(2,1)S(1)} fusion(bf16[2048,2048]{1,0:T(8,128)(2,1)S(1)} %fusion.29, bf16[4096,2048]{1,0:T(8,128)(2,1)} %param.11), kind=kOutput, calls=%fused_computation.78 | convolution fusion | flops 10740039680 | bytes 18874368 | tf_op jit(solution)/shard_map/tv,dv->td/dot_general | solution.py:169
  598.8 15.8 %collective-permute-done.43 = bf16[4,2,64,768]{3,2,1,0:T(8,128)(2,1)} collective-permute-done((bf16[4,2,64,768]{3,2,1,0:T(8,128)(2,1)}, bf16[4,2,64,768]{3,2,1,0:T(8,128)(2,1)}, u32[]{:S(2)}, u32[]{:S(2)}) %collective-permute-start.43) | collective-permute-done | bytes 786464 | tf_op jit(solution)/shard_map/ppermute | solution.py:52
  616.6 16.7 %collective-permute-done.42 = bf16[4,2,64,768]{3,2,1,0:T(8,128)(2,1)} collective-permute-done((bf16[4,2,64,768]{3,2,1,0:T(8,128)(2,1)}, bf16[4,2,64,768]{3,2,1,0:T(8,128)(2,1)}, u32[]{:S(2)}, u32[]{:S(2)}) %collective-permute-start.42) | collective-permute-done | bytes 786464 | tf_op jit(solution)/shard_map/ppermute | solution.py:52
  635.1 26.2 %collective-permute-done.37 = bf16[4,2,64,1280]{3,2,0,1:T(8,128)(2,1)} collective-permute-done((bf16[4,2,64,1280]{3,2,0,1:T(8,128)(2,1)}, bf16[4,2,64,1280]{3,2,0,1:T(8,128)(2,1)}, u32[]{:S(2)}, u32[]{:S(2)}) %collective-permute-start.37) | collective-permute-done | bytes 1310752 | tf_op jit(solution)/shard_map/ppermute | solution.py:52
  661.4 42.4 %fusion.68 = f32[4096,2048]{1,0:T(8,128)} fusion(bf16[2048,4096]{1,0:T(8,128)(2,1)} %all-gather.10.cloned.1.call-done, bf16[2048,2048]{1,0:T(8,128)(2,1)S(1)} %bitcast.273), kind=kOutput, calls=%fused_computation.352 | convolution fusion | flops 34359738368 | bytes 58720256 | tf_op jit(solution)/shard_map/td,tv->dv/dot_general | solution.py:175
  727.1 16.5 %collective-permute-start.53 = (f32[2,64,768]{2,1,0:T(8,128)}, f32[2,64,768]{2,1,0:T(8,128)}, u32[]{:S(2)}, u32[]{:S(2)}) collective-permute-start(f32[2,64,768]{2,1,0:T(8,128)} %get-tuple-element.444), channel_id=1, source_target_pairs={{0,8},{1,9},{2,10},{3,11},{4,12},{5,13},{6,14},{7,15},{8,0},{9,1},... | collective-permute-start | bytes 1179656 | tf_op jit(solution)/shard_map/ppermute | solution.py:52
  743.6 24.5 %collective-permute-done.57 = f32[2,64,768]{2,1,0:T(8,128)S(1)} collective-permute-done((f32[2,64,768]{2,1,0:T(8,128)S(1)}, f32[2,64,768]{2,1,0:T(8,128)S(1)}, u32[]{:S(2)}, u32[]{:S(2)}) %collective-permute-start.57) | collective-permute-done | bytes 393248 | tf_op jit(solution)/shard_map/ppermute | solution.py:52
  770.9 45.7 %add_convert_fusion = bf16[4096,2048]{1,0:T(8,128)(2,1)} fusion(f32[4096,2048]{1,0:T(8,128)} %fusion.68, bf16[2048,4096]{1,0:T(8,128)(2,1)} %all-gather.12.cloned.1.call-done, bf16[2048,2048]{1,0:T(8,128)(2,1)} %copy-done.11), kind=kOutput, calls=%fused_computation.63 | convolution fusion | flops 34376515584 | bytes 75497472 | tf_op jit(solution)/shard_map/td,tv->dv/dot_general | solution.py:175
  831.3 13.3 %collective-permute-start.61 = (f32[64,1280]{1,0:T(8,128)}, f32[64,1280]{1,0:T(8,128)S(1)}, u32[]{:S(2)}, u32[]{:S(2)}) collective-permute-start(f32[64,1280]{1,0:T(8,128)} %get-tuple-element.471), channel_id=1, source_target_pairs={{0,16},{1,17},{2,18},{3,19},{4,20},{5,21},{6,22},{7,23},{8,24},{9,... | collective-permute-start | bytes 983048 | tf_op jit(solution)/shard_map/ppermute | solution.py:52
  846.2 16.1 %collective-permute-done.64 = f32[64,1280]{1,0:T(8,128)} collective-permute-done((f32[64,1280]{1,0:T(8,128)}, f32[64,1280]{1,0:T(8,128)}, u32[]{:S(2)}, u32[]{:S(2)}) %collective-permute-start.64) | collective-permute-done | bytes 327712 | tf_op jit(solution)/shard_map/ppermute | solution.py:52
  868.8 18.0 %collective-permute-done.61 = f32[64,1280]{1,0:T(8,128)S(1)} collective-permute-done((f32[64,1280]{1,0:T(8,128)}, f32[64,1280]{1,0:T(8,128)S(1)}, u32[]{:S(2)}, u32[]{:S(2)}) %collective-permute-start.61) | collective-permute-done | bytes 327712 | tf_op jit(solution)/shard_map/ppermute | solution.py:52
  905.1 13.4 %collective-permute-done.72 = f32[64,1280]{1,0:T(8,128)S(1)} collective-permute-done((f32[64,1280]{1,0:T(8,128)S(1)}, f32[64,1280]{1,0:T(8,128)S(1)}, u32[]{:S(2)}, u32[]{:S(2)}) %collective-permute-start.72) | collective-permute-done | bytes 327712 | tf_op jit(solution)/shard_map/ppermute | solution.py:52
  918.5 12.2 %collective-permute-done.69 = f32[64,1280]{1,0:T(8,128)S(1)} collective-permute-done((f32[64,1280]{1,0:T(8,128)S(1)}, f32[64,1280]{1,0:T(8,128)S(1)}, u32[]{:S(2)}, u32[]{:S(2)}) %collective-permute-start.69) | collective-permute-done | bytes 327712 | tf_op jit(solution)/shard_map/ppermute | solution.py:52
  989.6 22.7 %conditional.1 = (f32[]{:T(128)}, bf16[3,64,4096]{2,1,0:T(8,128)(2,1)}, bf16[4096,2048]{1,0:T(8,128)(2,1)}, f32[4096]{0:T(1024)}) conditional(s32[]{:T(128)} %convert_element_type.476, (s32[3,64]{1,0:T(4,128)S(1)}, bf16[3,64,4096]{2,1,0:T(8,128)(2,1)S(1)}, f32[4096]{0:T(1024)S(1)}, bf16[4096,2048]{1,0:T(8,128)(2,1)}, ...), branch_computations={%region_17.31_spmd, %region_31.34_spmd} | conditional | flops 309563817984 | bytes 906139648 | solution.py:223
  (604 shorter events, 415.5 us)
Async XLA Ops:
  7.2 187.5 %all-gather.10.cloned.1.call-start = ((), (), s32[]{:S(2)}) async-start(), calls=%async_computation.2 | async-start | bytes 17301504 | tf_op jit(solution)/shard_map/all_gather | solution.py:99
  79.2 267.7 %all-gather.12.cloned.1.call-start = ((), (), s32[]{:S(2)}) async-start(), calls=%async_computation.3 | async-start | bytes 17301504 | tf_op jit(solution)/shard_map/all_gather | solution.py:99
  309.0 98.4 %collective-permute-start.15 = (bf16[4,2,64,768]{3,2,1,0:T(8,128)(2,1)}, bf16[4,2,64,768]{3,2,1,0:T(8,128)(2,1)}, u32[]{:S(2)}, u32[]{:S(2)}) collective-permute-start(bf16[4,2,64,768]{3,2,1,0:T(8,128)(2,1)} %get-tuple-element.466), channel_id=1, source_target_pairs={{0,1},{1,0},{2,3},{3,2},{4,5},{5,4},{6,7},{7,6},{8,9},{9,8},{10,11... | collective-permute-start | bytes 2359304 | tf_op jit(solution)/shard_map/ppermute | solution.py:52
  309.0 98.4 %collective-permute-start.14 = (bf16[4,2,64,768]{3,2,1,0:T(8,128)(2,1)}, bf16[4,2,64,768]{3,2,1,0:T(8,128)(2,1)}, u32[]{:S(2)}, u32[]{:S(2)}) collective-permute-start(bf16[4,2,64,768]{3,2,1,0:T(8,128)(2,1)} %get-tuple-element.467), channel_id=1, source_target_pairs={{0,3},{1,2},{2,1},{3,0},{4,7},{5,6},{6,5},{7,4},{8,11},{9,10},{10,... | collective-permute-start | bytes 2359304 | tf_op jit(solution)/shard_map/ppermute | solution.py:52
  310.6 96.7 %collective-permute-start.13 = (bf16[4,2,64,768]{3,2,1,0:T(8,128)(2,1)}, bf16[4,2,64,768]{3,2,1,0:T(8,128)(2,1)}, u32[]{:S(2)}, u32[]{:S(2)}) collective-permute-start(bf16[4,2,64,768]{3,2,1,0:T(8,128)(2,1)} %get-tuple-element.468), channel_id=1, source_target_pairs={{0,2},{1,3},{2,0},{3,1},{4,6},{5,7},{6,4},{7,5},{8,10},{9,11},{10,... | collective-permute-start | bytes 2359304 | tf_op jit(solution)/shard_map/ppermute | solution.py:52
  422.4 55.0 %collective-permute-start.31 = (bf16[4,2,64,1280]{3,2,0,1:T(8,128)(2,1)S(1)}, bf16[4,2,64,1280]{3,2,0,1:T(8,128)(2,1)}, u32[]{:S(2)}, u32[]{:S(2)}) collective-permute-start(bf16[4,2,64,1280]{3,2,0,1:T(8,128)(2,1)S(1)} %bitcast.291), channel_id=1, source_target_pairs={{0,3},{1,2},{2,1},{3,0},{4,7},{5,6},{6,5},{7,4},{8,11},{9,10},{10,... | collective-permute-start | bytes 3932168 | tf_op jit(solution)/shard_map/ppermute | solution.py:52
  477.4 59.4 %collective-permute-start.50 = (f32[2,64,768]{2,1,0:T(8,128)}, f32[2,64,768]{2,1,0:T(8,128)}, u32[]{:S(2)}, u32[]{:S(2)}) collective-permute-start(f32[2,64,768]{2,1,0:T(8,128)} %get-tuple-element.454), channel_id=1, source_target_pairs={{0,24},{1,25},{2,26},{3,27},{4,28},{5,29},{6,30},{7,31},{8,16},{9,... | collective-permute-start | bytes 1179656 | tf_op jit(solution)/shard_map/ppermute | solution.py:52
  478.1 59.8 %collective-permute-start.49 = (f32[2,64,768]{2,1,0:T(8,128)}, f32[2,64,768]{2,1,0:T(8,128)S(1)}, u32[]{:S(2)}, u32[]{:S(2)}) collective-permute-start(f32[2,64,768]{2,1,0:T(8,128)} %get-tuple-element.455), channel_id=1, source_target_pairs={{0,16},{1,17},{2,18},{3,19},{4,20},{5,21},{6,22},{7,23},{8,24},{9,... | collective-permute-start | bytes 1179656 | tf_op jit(solution)/shard_map/ppermute | solution.py:52
  567.6 65.7 %collective-permute-start.40 = (f32[4,64,1280]{2,1,0:T(8,128)}, f32[4,64,1280]{2,1,0:T(8,128)S(1)}, u32[]{:S(2)}, u32[]{:S(2)}) collective-permute-start(f32[4,64,1280]{2,1,0:T(8,128)} %get-tuple-element.420), channel_id=1, source_target_pairs={{0,2},{1,3},{2,0},{3,1},{4,6},{5,7},{6,4},{7,5},{8,10},{9,11},{10,... | collective-permute-start | bytes 3932168 | tf_op jit(solution)/shard_map/ppermute | solution.py:52
  568.3 66.0 %collective-permute-start.41 = (f32[4,64,1280]{2,1,0:T(8,128)}, f32[4,64,1280]{2,1,0:T(8,128)S(1)}, u32[]{:S(2)}, u32[]{:S(2)}) collective-permute-start(f32[4,64,1280]{2,1,0:T(8,128)} %get-tuple-element.418), channel_id=1, source_target_pairs={{0,4},{1,5},{2,6},{3,7},{4,0},{5,1},{6,2},{7,3},{8,12},{9,13},{10,... | collective-permute-start | bytes 3932168 | tf_op jit(solution)/shard_map/ppermute | solution.py:52
  575.2 58.1 %collective-permute-start.42 = (bf16[4,2,64,768]{3,2,1,0:T(8,128)(2,1)}, bf16[4,2,64,768]{3,2,1,0:T(8,128)(2,1)}, u32[]{:S(2)}, u32[]{:S(2)}) collective-permute-start(bf16[4,2,64,768]{3,2,1,0:T(8,128)(2,1)} %get-tuple-element.464), channel_id=1, source_target_pairs={{0,2},{1,3},{2,0},{3,1},{4,6},{5,7},{6,4},{7,5},{8,10},{9,11},{10,... | collective-permute-start | bytes 2359304 | tf_op jit(solution)/shard_map/ppermute | solution.py:52
  576.6 84.7 %collective-permute-start.37 = (bf16[4,2,64,1280]{3,2,0,1:T(8,128)(2,1)}, bf16[4,2,64,1280]{3,2,0,1:T(8,128)(2,1)}, u32[]{:S(2)}, u32[]{:S(2)}) collective-permute-start(bf16[4,2,64,1280]{3,2,0,1:T(8,128)(2,1)} %bitcast.258), channel_id=1, source_target_pairs={{0,2},{1,3},{2,0},{3,1},{4,6},{5,7},{6,4},{7,5},{8,10},{9,11},{10,... | collective-permute-start | bytes 3932168 | tf_op jit(solution)/shard_map/ppermute | solution.py:52
  614.7 98.1 %collective-permute-start.38 = (bf16[4,2,64,1280]{3,2,0,1:T(8,128)(2,1)S(1)}, bf16[4,2,64,1280]{3,2,0,1:T(8,128)(2,1)}, u32[]{:S(2)}, u32[]{:S(2)}) collective-permute-start(bf16[4,2,64,1280]{3,2,0,1:T(8,128)(2,1)S(1)} %bitcast.294), channel_id=1, source_target_pairs={{0,3},{1,2},{2,1},{3,0},{4,7},{5,6},{6,5},{7,4},{8,11},{9,10},{10,... | collective-permute-start | bytes 3932168 | tf_op jit(solution)/shard_map/ppermute | solution.py:52
  633.3 81.0 %collective-permute-start.39 = (bf16[4,2,64,1280]{3,2,0,1:T(8,128)(2,1)S(1)}, bf16[4,2,64,1280]{3,2,0,1:T(8,128)(2,1)}, u32[]{:S(2)}, u32[]{:S(2)}) collective-permute-start(bf16[4,2,64,1280]{3,2,0,1:T(8,128)(2,1)S(1)} %bitcast.293), channel_id=1, source_target_pairs={{0,1},{1,0},{2,3},{3,2},{4,5},{5,4},{6,7},{7,6},{8,9},{9,8},{10,11... | collective-permute-start | bytes 3932168 | tf_op jit(solution)/shard_map/ppermute | solution.py:52
  633.3 82.7 %collective-permute-start.34 = (bf16[4,2,64,1280]{3,2,0,1:T(8,128)(2,1)}, bf16[4,2,64,1280]{3,2,0,1:T(8,128)(2,1)}, u32[]{:S(2)}, u32[]{:S(2)}) collective-permute-start(bf16[4,2,64,1280]{3,2,0,1:T(8,128)(2,1)} %bitcast.255), channel_id=1, source_target_pairs={{0,4},{1,5},{2,6},{3,7},{4,0},{5,1},{6,2},{7,3},{8,12},{9,13},{10,... | collective-permute-start | bytes 3932168 | tf_op jit(solution)/shard_map/ppermute | solution.py:52
  634.3 86.7 %collective-permute-start.35 = (bf16[4,2,64,1280]{3,2,0,1:T(8,128)(2,1)}, bf16[4,2,64,1280]{3,2,0,1:T(8,128)(2,1)}, u32[]{:S(2)}, u32[]{:S(2)}) collective-permute-start(bf16[4,2,64,1280]{3,2,0,1:T(8,128)(2,1)} %bitcast.254), channel_id=1, source_target_pairs={{0,5},{1,4},{2,7},{3,6},{4,1},{5,0},{6,3},{7,2},{8,13},{9,12},{10,... | collective-permute-start | bytes 3932168 | tf_op jit(solution)/shard_map/ppermute | solution.py:52
  661.4 61.1 %collective-permute-start.36 = (bf16[4,2,64,1280]{3,2,0,1:T(8,128)(2,1)}, bf16[4,2,64,1280]{3,2,0,1:T(8,128)(2,1)}, u32[]{:S(2)}, u32[]{:S(2)}) collective-permute-start(bf16[4,2,64,1280]{3,2,0,1:T(8,128)(2,1)} %bitcast.253), channel_id=1, source_target_pairs={{0,1},{1,0},{2,3},{3,2},{4,5},{5,4},{6,7},{7,6},{8,9},{9,8},{10,11... | collective-permute-start | bytes 3932168 | tf_op jit(solution)/shard_map/ppermute | solution.py:52
  714.3 53.9 %collective-permute-start.57 = (f32[2,64,768]{2,1,0:T(8,128)S(1)}, f32[2,64,768]{2,1,0:T(8,128)S(1)}, u32[]{:S(2)}, u32[]{:S(2)}) collective-permute-start(f32[2,64,768]{2,1,0:T(8,128)S(1)} %get-tuple-element.439), channel_id=1, source_target_pairs={{0,16},{1,17},{2,18},{3,19},{4,20},{5,21},{6,22},{7,23},{8,24},{9,... | collective-permute-start | bytes 1179656 | tf_op jit(solution)/shard_map/ppermute | solution.py:52
  721.0 97.8 %collective-permute-start.55 = (f32[2,64,768]{2,1,0:T(8,128)}, f32[2,64,768]{2,1,0:T(8,128)}, u32[]{:S(2)}, u32[]{:S(2)}) collective-permute-start(f32[2,64,768]{2,1,0:T(8,128)} %get-tuple-element.442), channel_id=1, source_target_pairs={{0,24},{1,25},{2,26},{3,27},{4,28},{5,29},{6,30},{7,31},{8,16},{9,... | collective-permute-start | bytes 1179656 | tf_op jit(solution)/shard_map/ppermute | solution.py:52
  722.5 97.2 %collective-permute-start.54 = (f32[2,64,768]{2,1,0:T(8,128)}, f32[2,64,768]{2,1,0:T(8,128)}, u32[]{:S(2)}, u32[]{:S(2)}) collective-permute-start(f32[2,64,768]{2,1,0:T(8,128)} %get-tuple-element.443), channel_id=1, source_target_pairs={{0,16},{1,17},{2,18},{3,19},{4,20},{5,21},{6,22},{7,23},{8,24},{9,... | collective-permute-start | bytes 1179656 | tf_op jit(solution)/shard_map/ppermute | solution.py:52
  727.1 92.6 %collective-permute-start.53 = (f32[2,64,768]{2,1,0:T(8,128)}, f32[2,64,768]{2,1,0:T(8,128)}, u32[]{:S(2)}, u32[]{:S(2)}) collective-permute-start(f32[2,64,768]{2,1,0:T(8,128)} %get-tuple-element.444), channel_id=1, source_target_pairs={{0,8},{1,9},{2,10},{3,11},{4,12},{5,13},{6,14},{7,15},{8,0},{9,1},... | collective-permute-start | bytes 1179656 | tf_op jit(solution)/shard_map/ppermute | solution.py:52
  768.1 76.5 %collective-permute-start.51 = (f32[4,64,1280]{2,1,0:T(8,128)}, f32[4,64,1280]{2,1,0:T(8,128)}, u32[]{:S(2)}, u32[]{:S(2)}) collective-permute-start(f32[4,64,1280]{2,1,0:T(8,128)} %get-tuple-element.415), channel_id=1, source_target_pairs={{0,2},{1,3},{2,0},{3,1},{4,6},{5,7},{6,4},{7,5},{8,10},{9,11},{10,... | collective-permute-start | bytes 3932168 | tf_op jit(solution)/shard_map/ppermute | solution.py:52
  769.6 57.3 %collective-permute-start.52 = (f32[4,64,1280]{2,1,0:T(8,128)}, f32[4,64,1280]{2,1,0:T(8,128)}, u32[]{:S(2)}, u32[]{:S(2)}) collective-permute-start(f32[4,64,1280]{2,1,0:T(8,128)} %get-tuple-element.414), channel_id=1, source_target_pairs={{0,4},{1,5},{2,6},{3,7},{4,0},{5,1},{6,2},{7,3},{8,12},{9,13},{10,... | collective-permute-start | bytes 3932168 | tf_op jit(solution)/shard_map/ppermute | solution.py:52
  831.3 55.5 %collective-permute-start.61 = (f32[64,1280]{1,0:T(8,128)}, f32[64,1280]{1,0:T(8,128)S(1)}, u32[]{:S(2)}, u32[]{:S(2)}) collective-permute-start(f32[64,1280]{1,0:T(8,128)} %get-tuple-element.471), channel_id=1, source_target_pairs={{0,16},{1,17},{2,18},{3,19},{4,20},{5,21},{6,22},{7,23},{8,24},{9,... | collective-permute-start | bytes 983048 | tf_op jit(solution)/shard_map/ppermute | solution.py:52
  (169 other events, 3326.3 us)
Sparse Core Ops, SparseCore 0:
  79.3 115.3 all-gather.9
  197.6 113.4 all-gather.11
